TPU v7x, 32 devices: a whole 2x2x4 slice. The times are simulated.
32 devices in a mesh: row: 8 (over z, core), col: 4 (over y, x).
Axes of the slice: x: 2, y: 2, z: 4, core: 2. Of those that a mesh axis runs over, the one named last changes fastest.
Arguments:
- gate_input: bfloat16 [2, 512, 53248], P(None, 'col', 'row'), may hold values from -6 to 6
- up_input: bfloat16 [2, 512, 53248], P(None, 'col', 'row'), may hold values from -6 to 6
- down_weight: bfloat16 [53248, 16384], P('row', 'col'), may hold values from -0.02734375 to 0.02734375
Outputs:
- mixed: bfloat16 [2, 512, 16384], P(None, 'row', 'col')
All inputs are finite; a program needn't handle non-finite values.
Results may differ from a plain program's by a relative error of at most 0.0049.
Values may be sent and summed in bfloat16 or wider, within the bound.
A program may use at most 128 MiB of HBM per device.

v0:
```python
import jax
import jax.numpy as jnp
from jax import lax
from jax.sharding import PartitionSpec as P


def gated_hidden(gate_part, up_part):
    product = jax.nn.silu(gate_part.astype(jnp.float32)) * up_part.astype(jnp.float32)
    return product.astype(jnp.bfloat16)


def gathered_hidden(gate_part, up_part):
    return lax.all_gather(gated_hidden(gate_part, up_part), "col", axis=1, tiled=True)


def body(gate_input, up_input, down_weight):
    hidden_units = down_weight.shape[0]
    width = down_weight.shape[1]
    hidden = gathered_hidden(gate_input, up_input)
    seq_count = hidden.shape[0]
    seq_tokens = hidden.shape[1]
    flat = hidden.reshape(seq_count * seq_tokens, hidden_units)
    partial_value = jnp.dot(flat, down_weight, preferred_element_type=jnp.float32)
    partial_value = partial_value.reshape(seq_count, seq_tokens, width)
    mixed = lax.psum_scatter(partial_value, "row", scatter_dimension=1, tiled=True)
    return mixed.astype(jnp.bfloat16)


def solution(mesh):
    return jax.shard_map(
        body,
        mesh=mesh,
        in_specs=(P(None, "col", "row"), P(None, "col", "row"), P("row", "col")),
        out_specs=P(None, "row", "col"),
        check_vma=False,
    )
```

profile of v0, /device:TPU:0, one launch (start us, length us, event | category | flops | bytes accessed | tf_op | source)
XLA Modules:
  0.0 389.2 jit_solution(1998762316375179421)
XLA Ops:
  6.5 0.0 all-gather.2.cloned.1.call-start
  6.5 5.2 %fusion.6 = bf16[2,128,6656]{2,1,0:T(8,128)(2,1)} fusion(bf16[2,128,6656]{2,1,0:T(8,128)(2,1)} %param.4, bf16[2,128,6656]{2,1,0:T(8,128)(2,1)} %param.3), kind=kLoop, calls=%fused_computation.8 | loop fusion | flops 13631488 | bytes 10223616 | tf_op jit(solution)/shard_map/convert_element_type | solution.py:9
  11.7 0.0 all-gather.2.cloned.1.call-update
  11.7 0.0 reduce-scatter.2.cloned.1.call-start
  11.8 133.9 %all-gather.2.cloned.1.call-done = bf16[2,512,6656]{2,1,0:T(8,128)(2,1)} async-done(((bf16[2,128,6656]{2,1,0:T(8,128)(2,1)}), bf16[2,512,6656]{2,1,0:T(8,128)(2,1)}) %all-gather.2.cloned.1.call-update) | async-done | bytes 13631504 | tf_op jit(solution)/shard_map/all_gather | solution.py:13
  145.7 65.6 %fusion = f32[2,512,4096]{2,1,0:T(8,128)} fusion(bf16[2,512,6656]{2,1,0:T(8,128)(2,1)} %all-gather.2.cloned.1.call-done, bf16[6656,4096]{1,0:T(8,128)(2,1)} %param.5), kind=kOutput, calls=%fused_computation | convolution fusion | flops 55834574848 | bytes 84934656 | tf_op jit(solution)/shard_map/dot_general | solution.py:23
  211.3 0.0 reduce-scatter.2.cloned.1.call-update
  211.3 168.3 %reduce-scatter.2.cloned.1.call-done = f32[2,64,4096]{2,1,0:T(8,128)} async-done(((f32[2,512,4096]{2,1,0:T(8,128)}), f32[2,64,4096]{2,1,0:T(8,128)}) %reduce-scatter.2.cloned.1.call-update) | async-done | bytes 2097168 | tf_op jit(solution)/shard_map/reduce_scatter | solution.py:25
  379.7 2.7 convert_element_type.15
Async XLA Ops:
  6.5 139.2 %all-gather.2.cloned.1.call-start = ((), (), s32[]{:S(2)}) async-start(), calls=%async_computation.1 | async-start | bytes 17039360 | tf_op jit(solution)/shard_map/all_gather | solution.py:13
  11.7 367.9 %reduce-scatter.2.cloned.1.call-start = ((), (), s32[]{:S(2)}) async-start(), calls=%async_computation.2 | async-start | bytes 18874368 | tf_op jit(solution)/shard_map/reduce_scatter | solution.py:25
Sparse Core Ops, SparseCore 0:
  11.9 133.8 all-gather.1
  211.5 168.1 reduce-scatter.1
where the time goes:
time: 389 us
  waiting for transfers between devices  302 us (78%)
  matrix products  65.6 us (17%)
  between operations  13.4 us (3%)
  other arithmetic  7.86 us (2%)
    reduce_scatter x1, waiting for transfers between devices, body(): lax.psum_scatter(partial_value, 'row', scatter_dimension=1, tiled=True)  168 us
    all_gather x1, waiting for transfers between devices, gathered_hidden(): lax.all_gather(gated_hidden(gate_part, up_part), 'col', axis=1, tiled=True)  134 us
    dot_general x1, matrix products, body(): jnp.dot(flat, down_weight, preferred_element_type=jnp.float32)  65.6 us
  transfers between devices with their start and end apart: 2, of which 2 were waited for; matrix products, arithmetic and copies ran while one was open for 0% of the time, Pallas kernels for 0%

commit v1 on v0

v1 whole, which is shorter than its diff:
```python
import functools

import jax
import jax.numpy as jnp
from jax import lax
from jax.sharding import PartitionSpec as P

PIECES = 4
PERMUTE = True


def gated_hidden(gate_part, up_part):
    product = jax.nn.silu(gate_part.astype(jnp.float32)) * up_part.astype(jnp.float32)
    return product.astype(jnp.bfloat16)


def gather_by_permutes(part, n):
    me = lax.axis_index("col")

    def swap(value, bit):
        return lax.ppermute(value, "col", [(i, i ^ bit) for i in range(n)])

    half = part.shape[0] // 2
    near = swap(part, 1)
    far = swap(part, 2)
    top = swap(near[:half], 2)
    low = swap(far[half:], 1)
    blocks = jnp.zeros((n,) + part.shape, part.dtype)
    blocks = lax.dynamic_update_slice(blocks, part[None], (me, 0, 0))
    blocks = lax.dynamic_update_slice(blocks, near[None], (me ^ 1, 0, 0))
    blocks = lax.dynamic_update_slice(blocks, far[None], (me ^ 2, 0, 0))
    blocks = lax.dynamic_update_slice(blocks, top[None], (me ^ 3, 0, 0))
    return lax.dynamic_update_slice(blocks, low[None], (me ^ 3, half, 0))


def body(cols, rows, gate_input, up_input, down_weight):
    hidden_units, width = down_weight.shape
    seqs, held, _ = gate_input.shape
    owned = held * cols // rows
    per_seq = max(PIECES // seqs, 1)
    step = owned // per_seq
    groups = held // owned
    outs = []
    for seq in range(seqs):
        seq_outs = []
        for piece in range(per_seq):
            def cut(a):
                a = a[seq].reshape(groups, owned, hidden_units)
                return a[:, piece * step:(piece + 1) * step].reshape(groups * step, hidden_units)
            part = gated_hidden(cut(gate_input), cut(up_input))
            if PERMUTE and cols == 4:
                flat = gather_by_permutes(part, cols).reshape(cols * groups * step, hidden_units)
            else:
                flat = lax.all_gather(part, "col", axis=0, tiled=True)
            partial_value = jnp.dot(flat, down_weight, preferred_element_type=jnp.float32).astype(jnp.bfloat16)
            seq_outs.append(lax.psum_scatter(partial_value, "row", scatter_dimension=0, tiled=True))
        outs.append(jnp.concatenate(seq_outs, axis=0) if per_seq > 1 else seq_outs[0])
    return jnp.stack(outs, axis=0)


def solution(mesh):
    return jax.shard_map(
        functools.partial(body, mesh.shape["col"], mesh.shape["row"]),
        mesh=mesh,
        in_specs=(P(None, "col", "row"), P(None, "col", "row"), P("row", "col")),
        out_specs=P(None, "row", "col"),
        check_vma=False,
    )
```

time: 389 us -> 287 us (0.74)
  waiting for transfers between devices: 302 us -> 93.1 us
  local copies, waits for them, and re-layouts: 0 us -> 40.1 us
  matrix products: 65.6 us -> 101 us
  starting transfers between devices: 0.04 us -> 22.5 us
  other arithmetic: 7.86 us -> 16.1 us
    all_gather x1 -> x0, waiting for transfers between devices: 134 us -> none  [gathered_hidden(): lax.all_gather(gated_hidden(gate_part, up_part), 'col', axis=1, tiled=True)]
    reduce_scatter x1 -> x4, waiting for transfers between devices: 168 us -> 59.3 us  [body(): lax.psum_scatter(partial_value, 'row', scatter_dimension=0, tiled=True)]
    dot_general x1 -> x4, matrix products: 65.6 us -> 101 us  [body(): jnp.dot(flat, down_weight, preferred_element_type=jnp.float32)]
    ppermute x0 -> x16, waiting for transfers between devices: none -> 33.7 us  [swap(): return lax.ppermute(value, 'col', [(i, i ^ bit) for i in range(n)])]
    ppermute x0 -> x16, starting transfers between devices: none -> 22.1 us  [swap(): return lax.ppermute(value, 'col', [(i, i ^ bit) for i in range(n)])]
    dynamic_update_slice x0 -> x16, local copies, waits for them, and re-layouts: none -> 19.1 us  [the longest x4 5.45 us: gather_by_permutes(): blocks = lax.dynamic_update_slice(blocks, top[None], (me ^ 3, 0, 0))]
    slice x0 -> x10, local copies, waits for them, and re-layouts: none -> 12.4 us  [the longest x4 5.39 us: gather_by_permutes(): top = swap(near[:half], 2)]
    unnamed x0 -> x26, local copies, waits for them, and re-layouts: none -> 5.84 us
  transfers between devices with their start and end apart: 2 -> 20, of which waited for: 2 -> 6; matrix products, arithmetic and copies ran while one was open for 0% -> 50% of each run, Pallas kernels for 0% -> 0%
where the time goes in v1:
time: 287 us; the launch traced here: 286 us
  matrix products  101 us (35%)
  waiting for transfers between devices  93.1 us (32%)
  local copies, waits for them, and re-layouts  40.1 us (14%)
  starting transfers between devices  22.5 us (8%)
  other arithmetic  16.1 us (6%)
  between operations  13.4 us (5%)
    dot_general x4, matrix products, body(): jnp.dot(flat, down_weight, preferred_element_type=jnp.float32)  101 us
    reduce_scatter x4, waiting for transfers between devices, body(): lax.psum_scatter(partial_value, 'row', scatter_dimension=0, tiled=True)  59.3 us
    ppermute x16, waiting for transfers between devices, swap(): return lax.ppermute(value, 'col', [(i, i ^ bit) for i in range(n)])  33.7 us
    ppermute x16, starting transfers between devices, swap(): return lax.ppermute(value, 'col', [(i, i ^ bit) for i in range(n)])  22.1 us
    convert_element_type x4, other arithmetic, gated_hidden(): return product.astype(jnp.bfloat16)  7.15 us
    unnamed x26, local copies, waits for them, and re-layouts  5.84 us
  transfers between devices with their start and end apart: 20, of which 6 were waited for; matrix products, arithmetic and copies ran while one was open for 50% of the time, Pallas kernels for 0%

profile of v1, /device:TPU:0, one launch (start us, length us, event | category | flops | bytes accessed | tf_op | source)
XLA Modules:
  0.0 285.8 jit_solution(6508116744291009111)
XLA Ops:
  6.5 2.3 fusion.36
  10.3 1.7 fusion.24
  12.3 3.0 %collective-permute-start = (bf16[64,6656]{1,0:T(8,128)(2,1)}, bf16[64,6656]{1,0:T(8,128)(2,1)}, u32[]{:S(2)}, u32[]{:S(2)}) collective-permute-start(bf16[64,6656]{1,0:T(8,128)(2,1)} %fusion.24), channel_id=1, source_target_pairs={{0,1},{1,0},{2,3},{3,2},{4,5},{5,4},{6,7},{7,6},{8,9},{9,8},{10,11... | collective-permute-start | bytes 2555912 | tf_op jit(solution)/shard_map/ppermute | solution.py:21
  18.6 2.3 slice_convert_fusion.2
  20.9 1.7 fusion.8
  23.0 2.0 collective-permute-start.8
  25.0 2.4 fusion
  27.4 2.1 broadcast.64.clone.3
  37.8 1.6 collective-permute-start.9
  42.1 11.5 %collective-permute-done.4 = bf16[64,6656]{1,0:T(8,128)(2,1)} collective-permute-done((bf16[64,6656]{1,0:T(8,128)(2,1)}, bf16[64,6656]{1,0:T(8,128)(2,1)}, u32[]{:S(2)}, u32[]{:S(2)}) %collective-permute-start.4) | collective-permute-done | bytes 852000 | tf_op jit(solution)/shard_map/ppermute | solution.py:21
  53.6 2.1 collective-permute-start.13
  55.6 1.8 slice.90
  57.4 2.2 bitcast_dynamic-update-slice_fusion.7
  60.9 1.8 slice.91
  62.7 2.2 bitcast_dynamic-update-slice_fusion.6
  66.1 5.7 %collective-permute-done.8 = bf16[64,6656]{1,0:T(8,128)(2,1)} collective-permute-done((bf16[64,6656]{1,0:T(8,128)(2,1)}, bf16[64,6656]{1,0:T(8,128)(2,1)}, u32[]{:S(2)}, u32[]{:S(2)}) %collective-permute-start.8) | collective-permute-done | bytes 852000 | tf_op jit(solution)/shard_map/ppermute | solution.py:21
  71.8 2.0 collective-permute-start.3
  73.9 1.8 slice.94
  78.6 11.4 %collective-permute-done.12 = bf16[64,6656]{1,0:T(8,128)(2,1)S(1)} collective-permute-done((bf16[64,6656]{1,0:T(8,128)(2,1)S(1)}, bf16[64,6656]{1,0:T(8,128)(2,1)S(1)}, u32[]{:S(2)}, u32[]{:S(2)}) %collective-permute-start.12) | collective-permute-done | bytes 852000 | tf_op jit(solution)/shard_map/ppermute | solution.py:21
  90.0 2.0 collective-permute-start.7
  96.1 5.0 %collective-permute-done.2 = bf16[32,6656]{1,0:T(8,128)(2,1)S(1)} collective-permute-done((bf16[32,6656]{1,0:T(8,128)(2,1)S(1)}, bf16[32,6656]{1,0:T(8,128)(2,1)S(1)}, u32[]{:S(2)}, u32[]{:S(2)}) %collective-permute-start.2) | collective-permute-done | bytes 426016 | tf_op jit(solution)/shard_map/ppermute | solution.py:21
  102.0 2.0 collective-permute-start.14
  104.9 25.2 %convolution_convert_fusion.3 = bf16[256,4096]{1,0:T(8,128)(2,1)} fusion(bf16[256,6656]{1,0:T(8,128)(2,1)} %bitcast.10, bf16[6656,4096]{1,0:T(8,128)(2,1)} %param.5), kind=kOutput, calls=%fused_computation.3 | convolution fusion | flops 13959692288 | bytes 60030976 | tf_op jit(solution)/shard_map/dot_general | solution.py:55
  131.6 1.8 bitcast_dynamic-update-slice_fusion.13
  133.4 1.8 bitcast_dynamic-update-slice_fusion.12
  135.2 25.6 %convolution_convert_fusion.2 = bf16[256,4096]{1,0:T(8,128)(2,1)} fusion(bf16[256,6656]{1,0:T(8,128)(2,1)} %bitcast.225, bf16[6656,4096]{1,0:T(8,128)(2,1)} %param.5), kind=kOutput, calls=%fused_computation.2 | convolution fusion | flops 13959692288 | bytes 60030976 | tf_op jit(solution)/shard_map/dot_general | solution.py:55
  161.0 1.8 bitcast_dynamic-update-slice_fusion.11
  162.8 1.8 bitcast_dynamic-update-slice_fusion.10
  164.5 25.5 %convolution_convert_fusion.1 = bf16[256,4096]{1,0:T(8,128)(2,1)} fusion(bf16[256,6656]{1,0:T(8,128)(2,1)} %bitcast.226, bf16[6656,4096]{1,0:T(8,128)(2,1)} %param.5), kind=kOutput, calls=%fused_computation.1 | convolution fusion | flops 13959692288 | bytes 60030976 | tf_op jit(solution)/shard_map/dot_general | solution.py:55
  192.4 24.3 %convolution_convert_fusion = bf16[256,4096]{1,0:T(8,128)(2,1)} fusion(bf16[256,6656]{1,0:T(8,128)(2,1)S(1)} %bitcast.224, bf16[6656,4096]{1,0:T(8,128)(2,1)} %param.5), kind=kOutput, calls=%fused_computation | convolution fusion | flops 13959692288 | bytes 60030976 | tf_op jit(solution)/shard_map/dot_general | solution.py:55
  217.8 22.4 %reduce-scatter.9.cloned.1.call-done = bf16[32,4096]{1,0:T(8,128)(2,1)} async-done(((bf16[256,4096]{1,0:T(8,128)(2,1)}), bf16[32,4096]{1,0:T(8,128)(2,1)}) %reduce-scatter.9.cloned.1.call-update) | async-done | bytes 262160 | tf_op jit(solution)/shard_map/reduce_scatter | solution.py:56
  240.3 36.8 %reduce-scatter.11.cloned.1.call-done = bf16[32,4096]{1,0:T(8,128)(2,1)} async-done(((bf16[256,4096]{1,0:T(8,128)(2,1)}), bf16[32,4096]{1,0:T(8,128)(2,1)}) %reduce-scatter.11.cloned.1.call-update) | async-done | bytes 262160 | tf_op jit(solution)/shard_map/reduce_scatter | solution.py:56
  (85 shorter events, 34.8 us)
Async XLA Ops:
  6.5 3.0 %copy-start.12 = (bf16[2,128,6656]{2,1,0:T(8,128)(2,1)S(1)}, bf16[2,128,6656]{2,1,0:T(8,128)(2,1)}, u32[]{:S(2)}) copy-start(bf16[2,128,6656]{2,1,0:T(8,128)(2,1)} %param.4) | copy-start | bytes 10223620
  6.5 210.2 %reduce-scatter.5.cloned.1.call-start = ((), (), s32[]{:S(2)}) async-start(), calls=%async_computation.4 | async-start | bytes 2359296 | tf_op jit(solution)/shard_map/reduce_scatter | solution.py:56
  10.2 1.7 copy-start
  10.3 2.0 copy-start.2
  12.3 25.5 %collective-permute-start = (bf16[64,6656]{1,0:T(8,128)(2,1)}, bf16[64,6656]{1,0:T(8,128)(2,1)}, u32[]{:S(2)}, u32[]{:S(2)}) collective-permute-start(bf16[64,6656]{1,0:T(8,128)(2,1)} %fusion.24), channel_id=1, source_target_pairs={{0,1},{1,0},{2,3},{3,2},{4,5},{5,4},{6,7},{7,6},{8,9},{9,8},{10,11... | collective-permute-start | bytes 2555912 | tf_op jit(solution)/shard_map/ppermute | solution.py:21
  15.2 25.2 %collective-permute-start.1 = (bf16[64,6656]{1,0:T(8,128)(2,1)}, bf16[64,6656]{1,0:T(8,128)(2,1)}, u32[]{:S(2)}, u32[]{:S(2)}) collective-permute-start(bf16[64,6656]{1,0:T(8,128)(2,1)} %fusion.24), channel_id=1, source_target_pairs={{0,2},{1,3},{2,0},{3,1},{4,6},{5,7},{6,4},{7,5},{8,10},{9,11},{10,... | collective-permute-start | bytes 2555912 | tf_op jit(solution)/shard_map/ppermute | solution.py:21
  18.1 35.5 %collective-permute-start.4 = (bf16[64,6656]{1,0:T(8,128)(2,1)}, bf16[64,6656]{1,0:T(8,128)(2,1)}, u32[]{:S(2)}, u32[]{:S(2)}) collective-permute-start(bf16[64,6656]{1,0:T(8,128)(2,1)} %fusion.16), channel_id=1, source_target_pairs={{0,1},{1,0},{2,3},{3,2},{4,5},{5,4},{6,7},{7,6},{8,9},{9,8},{10,11... | collective-permute-start | bytes 2555912 | tf_op jit(solution)/shard_map/ppermute | solution.py:21
  18.6 42.2 %collective-permute-start.5 = (bf16[64,6656]{1,0:T(8,128)(2,1)}, bf16[64,6656]{1,0:T(8,128)(2,1)}, u32[]{:S(2)}, u32[]{:S(2)}) collective-permute-start(bf16[64,6656]{1,0:T(8,128)(2,1)} %fusion.16), channel_id=1, source_target_pairs={{0,2},{1,3},{2,0},{3,1},{4,6},{5,7},{6,4},{7,5},{8,10},{9,11},{10,... | collective-permute-start | bytes 2555912 | tf_op jit(solution)/shard_map/ppermute | solution.py:21
  20.9 1.7 copy-start.6
  20.9 2.1 copy-start.8
  23.0 48.9 %collective-permute-start.8 = (bf16[64,6656]{1,0:T(8,128)(2,1)}, bf16[64,6656]{1,0:T(8,128)(2,1)}, u32[]{:S(2)}, u32[]{:S(2)}) collective-permute-start(bf16[64,6656]{1,0:T(8,128)(2,1)} %fusion.8), channel_id=1, source_target_pairs={{0,1},{1,0},{2,3},{3,2},{4,5},{5,4},{6,7},{7,6},{8,9},{9,8},{10,11... | collective-permute-start | bytes 2555912 | tf_op jit(solution)/shard_map/ppermute | solution.py:21
  27.4 2.1 copy-start.1
  27.4 3.2 %copy-start.3 = (f32[2,32,6656]{2,1,0:T(8,128)S(1)}, f32[2,32,6656]{2,1,0:T(8,128)}, u32[]{:S(2)}) copy-start(f32[2,32,6656]{2,1,0:T(8,128)} %copy-done.2) | copy-start | bytes 5111812
  32.7 1.5 copy-start.7
  32.7 2.0 copy-start.9
  35.3 2.0 copy-start.5
  37.8 39.1 %collective-permute-start.9 = (bf16[64,6656]{1,0:T(8,128)(2,1)}, bf16[64,6656]{1,0:T(8,128)(2,1)S(1)}, u32[]{:S(2)}, u32[]{:S(2)}) collective-permute-start(bf16[64,6656]{1,0:T(8,128)(2,1)} %fusion.8), channel_id=1, source_target_pairs={{0,2},{1,3},{2,0},{3,1},{4,6},{5,7},{6,4},{7,5},{8,10},{9,11},{10,... | collective-permute-start | bytes 2555912 | tf_op jit(solution)/shard_map/ppermute | solution.py:21
  40.5 49.5 %collective-permute-start.12 = (bf16[64,6656]{1,0:T(8,128)(2,1)S(1)}, bf16[64,6656]{1,0:T(8,128)(2,1)S(1)}, u32[]{:S(2)}, u32[]{:S(2)}) collective-permute-start(bf16[64,6656]{1,0:T(8,128)(2,1)S(1)} %fusion), channel_id=1, source_target_pairs={{0,1},{1,0},{2,3},{3,2},{4,5},{5,4},{6,7},{7,6},{8,9},{9,8},{10,11... | collective-permute-start | bytes 2555912 | tf_op jit(solution)/shard_map/ppermute | solution.py:21
  53.6 38.5 %collective-permute-start.13 = (bf16[64,6656]{1,0:T(8,128)(2,1)S(1)}, bf16[64,6656]{1,0:T(8,128)(2,1)S(1)}, u32[]{:S(2)}, u32[]{:S(2)}) collective-permute-start(bf16[64,6656]{1,0:T(8,128)(2,1)S(1)} %fusion), channel_id=1, source_target_pairs={{0,2},{1,3},{2,0},{3,1},{4,6},{5,7},{6,4},{7,5},{8,10},{9,11},{10,... | collective-permute-start | bytes 2555912 | tf_op jit(solution)/shard_map/ppermute | solution.py:21
  60.9 40.3 %collective-permute-start.2 = (bf16[32,6656]{1,0:T(8,128)(2,1)S(1)}, bf16[32,6656]{1,0:T(8,128)(2,1)S(1)}, u32[]{:S(2)}, u32[]{:S(2)}) collective-permute-start(bf16[32,6656]{1,0:T(8,128)(2,1)S(1)} %slice.86), channel_id=1, source_target_pairs={{0,2},{1,3},{2,0},{3,1},{4,6},{5,7},{6,4},{7,5},{8,10},{9,11},{10,... | collective-permute-start | bytes 1277960 | tf_op jit(solution)/shard_map/ppermute | solution.py:21
  66.1 12.4 %copy-start.10 = (bf16[4,64,6656]{2,1,0:T(8,128)(2,1)}, bf16[4,64,6656]{2,1,0:T(8,128)(2,1)S(1)}, u32[]{:S(2)}) copy-start(bf16[4,64,6656]{2,1,0:T(8,128)(2,1)S(1)} %bitcast_dynamic-update-slice_fusion.4) | copy-start | bytes 10223620
  71.8 30.2 %collective-permute-start.3 = (bf16[32,6656]{1,0:T(8,128)(2,1)S(1)}, bf16[32,6656]{1,0:T(8,128)(2,1)S(1)}, u32[]{:S(2)}, u32[]{:S(2)}) collective-permute-start(bf16[32,6656]{1,0:T(8,128)(2,1)S(1)} %slice.87), channel_id=1, source_target_pairs={{0,1},{1,0},{2,3},{3,2},{4,5},{5,4},{6,7},{7,6},{8,9},{9,8},{10,11... | collective-permute-start | bytes 1277960 | tf_op jit(solution)/shard_map/ppermute | solution.py:21
  76.9 53.3 %collective-permute-start.6 = (bf16[32,6656]{1,0:T(8,128)(2,1)}, bf16[32,6656]{1,0:T(8,128)(2,1)}, u32[]{:S(2)}, u32[]{:S(2)}) collective-permute-start(bf16[32,6656]{1,0:T(8,128)(2,1)} %slice.90), channel_id=1, source_target_pairs={{0,2},{1,3},{2,0},{3,1},{4,6},{5,7},{6,4},{7,5},{8,10},{9,11},{10,... | collective-permute-start | bytes 1277960 | tf_op jit(solution)/shard_map/ppermute | solution.py:21
  78.5 16.0 %copy-start.11 = (bf16[4,64,6656]{2,1,0:T(8,128)(2,1)}, bf16[4,64,6656]{2,1,0:T(8,128)(2,1)S(1)}, u32[]{:S(2)}) copy-start(bf16[4,64,6656]{2,1,0:T(8,128)(2,1)S(1)} %bitcast_dynamic-update-slice_fusion.2) | copy-start | bytes 10223620
  90.0 43.4 %collective-permute-start.7 = (bf16[32,6656]{1,0:T(8,128)(2,1)}, bf16[32,6656]{1,0:T(8,128)(2,1)}, u32[]{:S(2)}, u32[]{:S(2)}) collective-permute-start(bf16[32,6656]{1,0:T(8,128)(2,1)} %slice.91), channel_id=1, source_target_pairs={{0,1},{1,0},{2,3},{3,2},{4,5},{5,4},{6,7},{7,6},{8,9},{9,8},{10,11... | collective-permute-start | bytes 1277960 | tf_op jit(solution)/shard_map/ppermute | solution.py:21
  92.1 68.9 %collective-permute-start.10 = (bf16[32,6656]{1,0:T(8,128)(2,1)}, bf16[32,6656]{1,0:T(8,128)(2,1)}, u32[]{:S(2)}, u32[]{:S(2)}) collective-permute-start(bf16[32,6656]{1,0:T(8,128)(2,1)} %slice.94), channel_id=1, source_target_pairs={{0,2},{1,3},{2,0},{3,1},{4,6},{5,7},{6,4},{7,5},{8,10},{9,11},{10,... | collective-permute-start | bytes 1277960 | tf_op jit(solution)/shard_map/ppermute | solution.py:21
  101.1 61.6 %collective-permute-start.11 = (bf16[32,6656]{1,0:T(8,128)(2,1)}, bf16[32,6656]{1,0:T(8,128)(2,1)}, u32[]{:S(2)}, u32[]{:S(2)}) collective-permute-start(bf16[32,6656]{1,0:T(8,128)(2,1)} %slice.95), channel_id=1, source_target_pairs={{0,1},{1,0},{2,3},{3,2},{4,5},{5,4},{6,7},{7,6},{8,9},{9,8},{10,11... | collective-permute-start | bytes 1277960 | tf_op jit(solution)/shard_map/ppermute | solution.py:21
  102.0 88.3 %collective-permute-start.14 = (bf16[32,6656]{1,0:T(8,128)(2,1)}, bf16[32,6656]{1,0:T(8,128)(2,1)}, u32[]{:S(2)}, u32[]{:S(2)}) collective-permute-start(bf16[32,6656]{1,0:T(8,128)(2,1)} %slice.98), channel_id=1, source_target_pairs={{0,2},{1,3},{2,0},{3,1},{4,6},{5,7},{6,4},{7,5},{8,10},{9,11},{10,... | collective-permute-start | bytes 1277960 | tf_op jit(solution)/shard_map/ppermute | solution.py:21
  130.1 86.6 %reduce-scatter.7.cloned.1.call-start = ((), (), s32[]{:S(2)}) async-start(), calls=%async_computation.5 | async-start | bytes 2359296 | tf_op jit(solution)/shard_map/reduce_scatter | solution.py:56
  130.2 61.2 %collective-permute-start.15 = (bf16[32,6656]{1,0:T(8,128)(2,1)}, bf16[32,6656]{1,0:T(8,128)(2,1)}, u32[]{:S(2)}, u32[]{:S(2)}) collective-permute-start(bf16[32,6656]{1,0:T(8,128)(2,1)} %slice.99), channel_id=1, source_target_pairs={{0,1},{1,0},{2,3},{3,2},{4,5},{5,4},{6,7},{7,6},{8,9},{9,8},{10,11... | collective-permute-start | bytes 1277960 | tf_op jit(solution)/shard_map/ppermute | solution.py:21
  160.9 79.4 %reduce-scatter.9.cloned.1.call-start = ((), (), s32[]{:S(2)}) async-start(), calls=%async_computation.6 | async-start | bytes 2359296 | tf_op jit(solution)/shard_map/reduce_scatter | solution.py:56
  190.0 87.1 %reduce-scatter.11.cloned.1.call-start = ((), (), s32[]{:S(2)}) async-start(), calls=%async_computation.7 | async-start | bytes 2359296 | tf_op jit(solution)/shard_map/reduce_scatter | solution.py:56
  (1 other events, 1.5 us)
Sparse Core Ops, SparseCore 0:
  130.2 36.2 reduce-scatter.4
  168.8 34.5 reduce-scatter.6
  205.7 34.5 reduce-scatter.8
  242.4 34.6 reduce-scatter.10
